TPU v7x, 32 devices: a whole 2x2x4 slice. The times are simulated.
32 devices in a mesh: cp: 16 (over z, x, core), tp: 2 (over y).
Axes of the slice: x: 2, y: 2, z: 4, core: 2. Of those that a mesh axis runs over, the one named last changes fastest.
Arguments:
- hidden: bfloat16 [8192, 4096], P('cp', 'tp'), may hold values from -6 to 6
- norm_gain: float32 [4096], replicated, may hold values from 0.5 to 1.5
- w_query: bfloat16 [4096, 4096], P(None, 'tp'), may hold values from -0.140625 to 0.140625
- w_key: bfloat16 [4096, 1024], P(None, 'tp'), may hold values from -4 to 4
- w_value: bfloat16 [4096, 1024], P(None, 'tp'), may hold values from -0.09375 to 0.09375
- w_out: bfloat16 [4096, 4096], P('tp'), may hold values from -0.5 to 0.5
- doc_ids: int32 [8192], P('cp'), may hold values from 0 to 5, never falling along the last dimension, each value on 1 to 6144 neighbouring positions
Outputs:
- updated: bfloat16 [8192, 4096], P('cp', 'tp')
Inputs may be any that keep to these rules, and one draw needn't show every extreme that they name: `doc_ids`: document numbers never fall along the sequence; every document has 1 to 6144 tokens.
All inputs are finite; a program needn't handle non-finite values.
Results may differ from a plain program's by a relative error of at most 0.017.
The roundings to bfloat16 on the way count: a program that leaves them out, or rounds other values in their place, can miss the bound.
Values may be sent and summed in bfloat16 or wider, within the bound.
A program may use at most 128 MiB of HBM per device.

v0:
```python
import jax
import jax.numpy as jnp
from jax import lax
from jax.sharding import PartitionSpec as P

HEADS = 32
KV_HEADS = 8
HEAD_SIZE = 128


epsilon = 1e-05
rope_base = 500000.0


def rotate(vectors, positions):
    half = HEAD_SIZE // 2
    freqs = rope_base ** (-jnp.arange(half, dtype=jnp.float32) * 2.0 / HEAD_SIZE)
    angles = positions.astype(jnp.float32)[:, None] * freqs[None, :]
    cosine = jnp.cos(angles)[:, None, :]
    sine = jnp.sin(angles)[:, None, :]
    first = vectors[..., :half]
    second = vectors[..., half:]
    return jnp.concatenate(
        [first * cosine - second * sine, second * cosine + first * sine], axis=-1
    )


def attend_block(
    loop_state, query_matrix, query_pos, query_doc, key_matrix, value_matrix, key_pos, key_doc
):
    best, total, running_output = loop_state
    logit_matrix = jnp.einsum(
        "ucpm,ycm->cpuy", query_matrix, key_matrix, preferred_element_type=jnp.float32
    ) * HEAD_SIZE ** (-0.5)
    allowed = (key_pos[None, :] <= query_pos[:, None]) & (key_doc[None, :] == query_doc[:, None])
    masked = jnp.where(allowed, logit_matrix, jnp.float32(-1e30))
    new_best = jnp.maximum(best, jnp.max(masked, axis=-1))
    correction_scale = jnp.exp(best - new_best)
    attention_weights = jnp.where(
        allowed, jnp.exp(logit_matrix - new_best[..., None]), jnp.float32(0.0)
    )
    total = total * correction_scale + jnp.sum(attention_weights, axis=-1)
    running_output = running_output * correction_scale[..., None] + jnp.einsum(
        "sfec,csh->sfeh",
        attention_weights.astype(jnp.bfloat16),
        value_matrix,
        preferred_element_type=jnp.float32,
    )
    return (new_best, total, running_output)


def shards(hidden, norm_gain, w_query, w_key, w_value, w_out, doc_ids):
    tok_rows = hidden.shape[0]
    half_rows = tok_rows // 2
    width = norm_gain.shape[0]
    group = HEADS // KV_HEADS
    local_kv = w_key.shape[1] // HEAD_SIZE
    query_cols = w_query.shape[1]
    key_cols = w_key.shape[1]
    wide_local = hidden.astype(jnp.float32)
    squares = lax.psum(jnp.sum(wide_local * wide_local, axis=1), "tp")
    inverse_rms = lax.rsqrt(squares / width + epsilon)[:, None]
    piece = lax.all_gather(hidden, "tp", axis=1, tiled=True)
    normed_piece = (piece.astype(jnp.float32) * inverse_rms * norm_gain[None, :]).astype(
        jnp.bfloat16
    )
    projected = jnp.concatenate(
        [
            jnp.dot(normed_piece, w_query, preferred_element_type=jnp.float32),
            jnp.dot(normed_piece, w_key, preferred_element_type=jnp.float32),
            jnp.dot(normed_piece, w_value, preferred_element_type=jnp.float32),
        ],
        axis=1,
    )
    cp_rank = lax.axis_index("cp")
    positions = cp_rank * tok_rows + jnp.arange(tok_rows, dtype=jnp.int32)
    query_raw = projected[:, :query_cols].reshape(tok_rows, local_kv * group, HEAD_SIZE)
    key_raw = projected[:, query_cols : query_cols + key_cols].reshape(
        tok_rows, local_kv, HEAD_SIZE
    )
    query_matrix = (
        rotate(query_raw, positions)
        .astype(jnp.bfloat16)
        .reshape(tok_rows, local_kv, group, HEAD_SIZE)
    )
    keys_flat = rotate(key_raw, positions).astype(jnp.bfloat16).reshape(tok_rows, key_cols)
    values_flat = projected[:, query_cols + key_cols :].astype(jnp.bfloat16)
    query_doc = doc_ids.astype(jnp.float32)
    docs_flat = query_doc.astype(jnp.bfloat16)
    first_queries = query_matrix[:half_rows]
    first_pos = positions[:half_rows]
    first_doc = query_doc[:half_rows]
    second_queries = query_matrix[half_rows:]
    second_doc = query_doc[half_rows:]
    second_start = cp_rank * tok_rows + half_rows
    second_pos = second_start + jnp.arange(half_rows, dtype=jnp.int32)
    last_first = cp_rank * tok_rows + half_rows - 1
    last_second = second_start + half_rows - 1
    init_half = (
        jnp.full((local_kv, group, half_rows), -1e30, jnp.float32),
        jnp.zeros((local_kv, group, half_rows), jnp.float32),
        jnp.zeros((local_kv, group, half_rows, HEAD_SIZE), jnp.float32),
    )
    init = (init_half, init_half)
    key_piece = lax.all_gather(keys_flat, "cp", axis=0, tiled=True)
    value_piece = lax.all_gather(values_flat, "cp", axis=0, tiled=True)
    doc_piece = lax.all_gather(docs_flat, "cp", axis=0, tiled=True)
    count = key_piece.shape[0]

    def inner(index, state):
        first_state, second_state = state
        offset = index * tok_rows
        key_blk = lax.dynamic_slice_in_dim(key_piece, offset, tok_rows, 0).reshape(
            tok_rows, local_kv, HEAD_SIZE
        )
        value_blk = lax.dynamic_slice_in_dim(value_piece, offset, tok_rows, 0).reshape(
            tok_rows, local_kv, HEAD_SIZE
        )
        key_doc = lax.dynamic_slice_in_dim(doc_piece, offset, tok_rows, 0).astype(jnp.float32)
        key_pos = offset + jnp.arange(tok_rows, dtype=jnp.int32)

        def attend_first(inner_state):
            return attend_block(
                inner_state,
                first_queries,
                first_pos,
                first_doc,
                key_blk,
                value_blk,
                key_pos,
                key_doc,
            )

        def attend_second(inner_state):
            return attend_block(
                inner_state,
                second_queries,
                second_pos,
                second_doc,
                key_blk,
                value_blk,
                key_pos,
                key_doc,
            )

        first_state = lax.cond(
            offset <= last_first, attend_first, lambda inner_state: inner_state, first_state
        )
        second_state = lax.cond(
            offset <= last_second, attend_second, lambda inner_state: inner_state, second_state
        )
        return (first_state, second_state)

    final = lax.fori_loop(0, count // tok_rows, inner, init)

    def finish(state):
        result = state[2] / state[1][..., None]
        return (
            jnp.transpose(result, (2, 0, 1, 3)).reshape(half_rows, query_cols).astype(jnp.bfloat16)
        )

    attended_first = finish(final[0])
    attended_second = finish(final[1])
    attended = jnp.concatenate([attended_first, attended_second], axis=0)
    terms = jnp.dot(attended, w_out, preferred_element_type=jnp.float32)
    summed = lax.psum_scatter(terms.astype(jnp.bfloat16), "tp", scatter_dimension=1, tiled=True)
    return summed


def solution(mesh):
    in_specs = (
        P("cp", "tp"),
        P(),
        P(None, "tp"),
        P(None, "tp"),
        P(None, "tp"),
        P("tp", None),
        P("cp"),
    )
    out_specs = P("cp", "tp")
    return jax.shard_map(shards, mesh=mesh, in_specs=in_specs, out_specs=out_specs, check_vma=False)
```

profile of v0, /device:TPU:26, one launch (start us, length us, event | category | flops | bytes accessed | tf_op | source)
XLA Modules:
  0.0 620.5 jit_solution(9094426565222155319)
XLA Ops:
  14.9 51.7 %all-gather.5.cloned.1.call-done = bf16[512,4096]{1,0:T(8,128)(2,1)} async-done(((bf16[512,2048]{1,0:T(8,128)(2,1)}), bf16[512,4096]{1,0:T(8,128)(2,1)}) %all-gather.5.cloned.1.call-update) | async-done | bytes 4194320 | tf_op jit(solution)/shard_map/all_gather | solution.py:63
  80.7 17.4 %all-gather = bf16[16,1,512]{2,1,0:T(2,128)(2,1)S(1)} all-gather(bf16[1,1,512]{2,1,0:T(2,128)(2,1)S(1)} %reshape.106), channel_id=1, replica_groups=mesh['cp'=16,'tp'=2] {'cp'}, dimensions={0}, use_global_device_ids=true | all-gather | bytes 17408 | tf_op jit(solution)/shard_map/all_gather | solution.py:107
  98.2 13.1 %convolution_bitcast_fusion = f32[64,8,16,128]{3,1,2,0:T(8,128)S(1)} fusion(bf16[4096,2048]{1,0:T(8,128)(2,1)} %param.15, bf16[512,4096]{1,0:T(8,128)(2,1)} %all-gather.5.cloned.1.call-done, f32[4096]{0:T(1024)S(1)} %copy-done.7, f32[512]{0:T(512)S(1)} %add_rsqrt_fusion), kind=kOutput, calls=%fused_computation.53 | convolution fusion | flops 8598323200 | bytes 25184256 | tf_op jit(solution)/shard_map/dot_general | solution.py:69
  115.5 33.4 %all-gather.7.cloned.1.call-done = bf16[8192,512]{0,1:T(8,128)(2,1)} async-done(((bf16[512,512]{0,1:T(8,128)(2,1)}), bf16[8192,512]{0,1:T(8,128)(2,1)}) %all-gather.7.cloned.1.call-update) | async-done | bytes 8388624 | tf_op jit(solution)/shard_map/all_gather | solution.py:105
  148.9 75.2 %all-gather.9.cloned.1.call-done = bf16[8192,512]{1,0:T(8,128)(2,1)} async-done(((bf16[512,512]{1,0:T(8,128)(2,1)}), bf16[8192,512]{1,0:T(8,128)(2,1)}) %all-gather.9.cloned.1.call-update) | async-done | bytes 8388624 | tf_op jit(solution)/shard_map/all_gather | solution.py:106
  227.2 294.4 %while.24 = (s32[]{:T(128)}, f32[4,4,256]{2,1,0:T(4,128)S(1)}, f32[4,4,256]{2,1,0:T(4,128)S(1)}, f32[4,4,256,128]{3,2,1,0:T(8,128)}, f32[4,4,256]{2,1,0:T(4,128)...) while((s32[]{:T(128)}, f32[4,4,256]{2,1,0:T(4,128)S(1)}, ...), condition=%wide.region_11.12_spmd.clone, body=%wide.region_2.11_spmd.clone.sunk | while | flops 2196522240 | bytes 105403112 | solution.py:154
  238.5 8.1 %conditional.7 = ((f32[4,4,256]{2,1,0:T(4,128)S(1)}, f32[4,4,256]{2,1,0:T(4,128)S(1)}, f32[4,4,256,128]{3,2,1,0:T(8,128)})) conditional(s32[]{:T(128)} %convert_element_type.129, (f32[4,4,256]{2,1,0:T(4,128)S(1)}, f32[4,4,256]{2,1,0:T(4,128)S(1)}, f32[4,4,256,128]{3,2,1,0:T(8,128)}) %tuple.74, (s32[512]{0:T(512)S(1)}, s32[]{:T(128)}, ...), branch_computations={%region_7.7_spmd, %region_8.10_spmd} | conditional | flops 1098260736 | bytes 51126392 | solution.py:149
  249.8 8.1 %conditional.6 = ((f32[4,4,256]{2,1,0:T(4,128)S(1)}, f32[4,4,256]{2,1,0:T(4,128)S(1)}, f32[4,4,256,128]{3,2,1,0:T(8,128)})) conditional(s32[]{:T(128)} %convert_element_type.128, (f32[4,4,256]{2,1,0:T(4,128)S(1)}, f32[4,4,256]{2,1,0:T(4,128)S(1)}, f32[4,4,256,128]{3,2,1,0:T(8,128)}) %tuple.72, (s32[512]{0:T(512)S(1)}, s32[256]{0:T(256)S(1)}, ...), branch_computations={%region_3.0_spmd, %region_4.6_spmd} | conditional | flops 1098260480 | bytes 51124340 | solution.py:146
  257.9 8.1 %conditional.7 = ((f32[4,4,256]{2,1,0:T(4,128)S(1)}, f32[4,4,256]{2,1,0:T(4,128)S(1)}, f32[4,4,256,128]{3,2,1,0:T(8,128)})) conditional(s32[]{:T(128)} %convert_element_type.129, (f32[4,4,256]{2,1,0:T(4,128)S(1)}, f32[4,4,256]{2,1,0:T(4,128)S(1)}, f32[4,4,256,128]{3,2,1,0:T(8,128)}) %tuple.74, (s32[512]{0:T(512)S(1)}, s32[]{:T(128)}, ...), branch_computations={%region_7.7_spmd, %region_8.10_spmd} | conditional | flops 1098260736 | bytes 51126392 | solution.py:149
  269.2 8.1 %conditional.6 = ((f32[4,4,256]{2,1,0:T(4,128)S(1)}, f32[4,4,256]{2,1,0:T(4,128)S(1)}, f32[4,4,256,128]{3,2,1,0:T(8,128)})) conditional(s32[]{:T(128)} %convert_element_type.128, (f32[4,4,256]{2,1,0:T(4,128)S(1)}, f32[4,4,256]{2,1,0:T(4,128)S(1)}, f32[4,4,256,128]{3,2,1,0:T(8,128)}) %tuple.72, (s32[512]{0:T(512)S(1)}, s32[256]{0:T(256)S(1)}, ...), branch_computations={%region_3.0_spmd, %region_4.6_spmd} | conditional | flops 1098260480 | bytes 51124340 | solution.py:146
  277.3 8.1 %conditional.7 = ((f32[4,4,256]{2,1,0:T(4,128)S(1)}, f32[4,4,256]{2,1,0:T(4,128)S(1)}, f32[4,4,256,128]{3,2,1,0:T(8,128)})) conditional(s32[]{:T(128)} %convert_element_type.129, (f32[4,4,256]{2,1,0:T(4,128)S(1)}, f32[4,4,256]{2,1,0:T(4,128)S(1)}, f32[4,4,256,128]{3,2,1,0:T(8,128)}) %tuple.74, (s32[512]{0:T(512)S(1)}, s32[]{:T(128)}, ...), branch_computations={%region_7.7_spmd, %region_8.10_spmd} | conditional | flops 1098260736 | bytes 51126392 | solution.py:149
  288.6 8.1 %conditional.6 = ((f32[4,4,256]{2,1,0:T(4,128)S(1)}, f32[4,4,256]{2,1,0:T(4,128)S(1)}, f32[4,4,256,128]{3,2,1,0:T(8,128)})) conditional(s32[]{:T(128)} %convert_element_type.128, (f32[4,4,256]{2,1,0:T(4,128)S(1)}, f32[4,4,256]{2,1,0:T(4,128)S(1)}, f32[4,4,256,128]{3,2,1,0:T(8,128)}) %tuple.72, (s32[512]{0:T(512)S(1)}, s32[256]{0:T(256)S(1)}, ...), branch_computations={%region_3.0_spmd, %region_4.6_spmd} | conditional | flops 1098260480 | bytes 51124340 | solution.py:146
  296.7 8.1 %conditional.7 = ((f32[4,4,256]{2,1,0:T(4,128)S(1)}, f32[4,4,256]{2,1,0:T(4,128)S(1)}, f32[4,4,256,128]{3,2,1,0:T(8,128)})) conditional(s32[]{:T(128)} %convert_element_type.129, (f32[4,4,256]{2,1,0:T(4,128)S(1)}, f32[4,4,256]{2,1,0:T(4,128)S(1)}, f32[4,4,256,128]{3,2,1,0:T(8,128)}) %tuple.74, (s32[512]{0:T(512)S(1)}, s32[]{:T(128)}, ...), branch_computations={%region_7.7_spmd, %region_8.10_spmd} | conditional | flops 1098260736 | bytes 51126392 | solution.py:149
  316.1 8.1 %conditional.7 = ((f32[4,4,256]{2,1,0:T(4,128)S(1)}, f32[4,4,256]{2,1,0:T(4,128)S(1)}, f32[4,4,256,128]{3,2,1,0:T(8,128)})) conditional(s32[]{:T(128)} %convert_element_type.129, (f32[4,4,256]{2,1,0:T(4,128)S(1)}, f32[4,4,256]{2,1,0:T(4,128)S(1)}, f32[4,4,256,128]{3,2,1,0:T(8,128)}) %tuple.74, (s32[512]{0:T(512)S(1)}, s32[]{:T(128)}, ...), branch_computations={%region_7.7_spmd, %region_8.10_spmd} | conditional | flops 1098260736 | bytes 51126392 | solution.py:149
  335.5 8.1 %conditional.7 = ((f32[4,4,256]{2,1,0:T(4,128)S(1)}, f32[4,4,256]{2,1,0:T(4,128)S(1)}, f32[4,4,256,128]{3,2,1,0:T(8,128)})) conditional(s32[]{:T(128)} %convert_element_type.129, (f32[4,4,256]{2,1,0:T(4,128)S(1)}, f32[4,4,256]{2,1,0:T(4,128)S(1)}, f32[4,4,256,128]{3,2,1,0:T(8,128)}) %tuple.74, (s32[512]{0:T(512)S(1)}, s32[]{:T(128)}, ...), branch_computations={%region_7.7_spmd, %region_8.10_spmd} | conditional | flops 1098260736 | bytes 51126392 | solution.py:149
  346.9 8.1 %conditional.6 = ((f32[4,4,256]{2,1,0:T(4,128)S(1)}, f32[4,4,256]{2,1,0:T(4,128)S(1)}, f32[4,4,256,128]{3,2,1,0:T(8,128)})) conditional(s32[]{:T(128)} %convert_element_type.128, (f32[4,4,256]{2,1,0:T(4,128)S(1)}, f32[4,4,256]{2,1,0:T(4,128)S(1)}, f32[4,4,256,128]{3,2,1,0:T(8,128)}) %tuple.72, (s32[512]{0:T(512)S(1)}, s32[256]{0:T(256)S(1)}, ...), branch_computations={%region_3.0_spmd, %region_4.6_spmd} | conditional | flops 1098260480 | bytes 51124340 | solution.py:146
  354.9 8.1 %conditional.7 = ((f32[4,4,256]{2,1,0:T(4,128)S(1)}, f32[4,4,256]{2,1,0:T(4,128)S(1)}, f32[4,4,256,128]{3,2,1,0:T(8,128)})) conditional(s32[]{:T(128)} %convert_element_type.129, (f32[4,4,256]{2,1,0:T(4,128)S(1)}, f32[4,4,256]{2,1,0:T(4,128)S(1)}, f32[4,4,256,128]{3,2,1,0:T(8,128)}) %tuple.74, (s32[512]{0:T(512)S(1)}, s32[]{:T(128)}, ...), branch_computations={%region_7.7_spmd, %region_8.10_spmd} | conditional | flops 1098260736 | bytes 51126392 | solution.py:149
  374.3 8.1 %conditional.7 = ((f32[4,4,256]{2,1,0:T(4,128)S(1)}, f32[4,4,256]{2,1,0:T(4,128)S(1)}, f32[4,4,256,128]{3,2,1,0:T(8,128)})) conditional(s32[]{:T(128)} %convert_element_type.129, (f32[4,4,256]{2,1,0:T(4,128)S(1)}, f32[4,4,256]{2,1,0:T(4,128)S(1)}, f32[4,4,256,128]{3,2,1,0:T(8,128)}) %tuple.74, (s32[512]{0:T(512)S(1)}, s32[]{:T(128)}, ...), branch_computations={%region_7.7_spmd, %region_8.10_spmd} | conditional | flops 1098260736 | bytes 51126392 | solution.py:149
  393.7 8.1 %conditional.7 = ((f32[4,4,256]{2,1,0:T(4,128)S(1)}, f32[4,4,256]{2,1,0:T(4,128)S(1)}, f32[4,4,256,128]{3,2,1,0:T(8,128)})) conditional(s32[]{:T(128)} %convert_element_type.129, (f32[4,4,256]{2,1,0:T(4,128)S(1)}, f32[4,4,256]{2,1,0:T(4,128)S(1)}, f32[4,4,256,128]{3,2,1,0:T(8,128)}) %tuple.74, (s32[512]{0:T(512)S(1)}, s32[]{:T(128)}, ...), branch_computations={%region_7.7_spmd, %region_8.10_spmd} | conditional | flops 1098260736 | bytes 51126392 | solution.py:149
  405.1 8.1 %conditional.6 = ((f32[4,4,256]{2,1,0:T(4,128)S(1)}, f32[4,4,256]{2,1,0:T(4,128)S(1)}, f32[4,4,256,128]{3,2,1,0:T(8,128)})) conditional(s32[]{:T(128)} %convert_element_type.128, (f32[4,4,256]{2,1,0:T(4,128)S(1)}, f32[4,4,256]{2,1,0:T(4,128)S(1)}, f32[4,4,256,128]{3,2,1,0:T(8,128)}) %tuple.72, (s32[512]{0:T(512)S(1)}, s32[256]{0:T(256)S(1)}, ...), branch_computations={%region_3.0_spmd, %region_4.6_spmd} | conditional | flops 1098260480 | bytes 51124340 | solution.py:146
  413.1 8.1 %conditional.7 = ((f32[4,4,256]{2,1,0:T(4,128)S(1)}, f32[4,4,256]{2,1,0:T(4,128)S(1)}, f32[4,4,256,128]{3,2,1,0:T(8,128)})) conditional(s32[]{:T(128)} %convert_element_type.129, (f32[4,4,256]{2,1,0:T(4,128)S(1)}, f32[4,4,256]{2,1,0:T(4,128)S(1)}, f32[4,4,256,128]{3,2,1,0:T(8,128)}) %tuple.74, (s32[512]{0:T(512)S(1)}, s32[]{:T(128)}, ...), branch_computations={%region_7.7_spmd, %region_8.10_spmd} | conditional | flops 1098260736 | bytes 51126392 | solution.py:149
  424.5 8.1 %conditional.6 = ((f32[4,4,256]{2,1,0:T(4,128)S(1)}, f32[4,4,256]{2,1,0:T(4,128)S(1)}, f32[4,4,256,128]{3,2,1,0:T(8,128)})) conditional(s32[]{:T(128)} %convert_element_type.128, (f32[4,4,256]{2,1,0:T(4,128)S(1)}, f32[4,4,256]{2,1,0:T(4,128)S(1)}, f32[4,4,256,128]{3,2,1,0:T(8,128)}) %tuple.72, (s32[512]{0:T(512)S(1)}, s32[256]{0:T(256)S(1)}, ...), branch_computations={%region_3.0_spmd, %region_4.6_spmd} | conditional | flops 1098260480 | bytes 51124340 | solution.py:146
  432.6 8.1 %conditional.7 = ((f32[4,4,256]{2,1,0:T(4,128)S(1)}, f32[4,4,256]{2,1,0:T(4,128)S(1)}, f32[4,4,256,128]{3,2,1,0:T(8,128)})) conditional(s32[]{:T(128)} %convert_element_type.129, (f32[4,4,256]{2,1,0:T(4,128)S(1)}, f32[4,4,256]{2,1,0:T(4,128)S(1)}, f32[4,4,256,128]{3,2,1,0:T(8,128)}) %tuple.74, (s32[512]{0:T(512)S(1)}, s32[]{:T(128)}, ...), branch_computations={%region_7.7_spmd, %region_8.10_spmd} | conditional | flops 1098260736 | bytes 51126392 | solution.py:149
  452.0 8.1 %conditional.7 = ((f32[4,4,256]{2,1,0:T(4,128)S(1)}, f32[4,4,256]{2,1,0:T(4,128)S(1)}, f32[4,4,256,128]{3,2,1,0:T(8,128)})) conditional(s32[]{:T(128)} %convert_element_type.129, (f32[4,4,256]{2,1,0:T(4,128)S(1)}, f32[4,4,256]{2,1,0:T(4,128)S(1)}, f32[4,4,256,128]{3,2,1,0:T(8,128)}) %tuple.74, (s32[512]{0:T(512)S(1)}, s32[]{:T(128)}, ...), branch_computations={%region_7.7_spmd, %region_8.10_spmd} | conditional | flops 1098260736 | bytes 51126392 | solution.py:149
  463.3 8.1 %conditional.6 = ((f32[4,4,256]{2,1,0:T(4,128)S(1)}, f32[4,4,256]{2,1,0:T(4,128)S(1)}, f32[4,4,256,128]{3,2,1,0:T(8,128)})) conditional(s32[]{:T(128)} %convert_element_type.128, (f32[4,4,256]{2,1,0:T(4,128)S(1)}, f32[4,4,256]{2,1,0:T(4,128)S(1)}, f32[4,4,256,128]{3,2,1,0:T(8,128)}) %tuple.72, (s32[512]{0:T(512)S(1)}, s32[256]{0:T(256)S(1)}, ...), branch_computations={%region_3.0_spmd, %region_4.6_spmd} | conditional | flops 1098260480 | bytes 51124340 | solution.py:146
  471.4 8.1 %conditional.7 = ((f32[4,4,256]{2,1,0:T(4,128)S(1)}, f32[4,4,256]{2,1,0:T(4,128)S(1)}, f32[4,4,256,128]{3,2,1,0:T(8,128)})) conditional(s32[]{:T(128)} %convert_element_type.129, (f32[4,4,256]{2,1,0:T(4,128)S(1)}, f32[4,4,256]{2,1,0:T(4,128)S(1)}, f32[4,4,256,128]{3,2,1,0:T(8,128)}) %tuple.74, (s32[512]{0:T(512)S(1)}, s32[]{:T(128)}, ...), branch_computations={%region_7.7_spmd, %region_8.10_spmd} | conditional | flops 1098260736 | bytes 51126392 | solution.py:149
  482.7 8.1 %conditional.6 = ((f32[4,4,256]{2,1,0:T(4,128)S(1)}, f32[4,4,256]{2,1,0:T(4,128)S(1)}, f32[4,4,256,128]{3,2,1,0:T(8,128)})) conditional(s32[]{:T(128)} %convert_element_type.128, (f32[4,4,256]{2,1,0:T(4,128)S(1)}, f32[4,4,256]{2,1,0:T(4,128)S(1)}, f32[4,4,256,128]{3,2,1,0:T(8,128)}) %tuple.72, (s32[512]{0:T(512)S(1)}, s32[256]{0:T(256)S(1)}, ...), branch_computations={%region_3.0_spmd, %region_4.6_spmd} | conditional | flops 1098260480 | bytes 51124340 | solution.py:146
  490.8 8.1 %conditional.7 = ((f32[4,4,256]{2,1,0:T(4,128)S(1)}, f32[4,4,256]{2,1,0:T(4,128)S(1)}, f32[4,4,256,128]{3,2,1,0:T(8,128)})) conditional(s32[]{:T(128)} %convert_element_type.129, (f32[4,4,256]{2,1,0:T(4,128)S(1)}, f32[4,4,256]{2,1,0:T(4,128)S(1)}, f32[4,4,256,128]{3,2,1,0:T(8,128)}) %tuple.74, (s32[512]{0:T(512)S(1)}, s32[]{:T(128)}, ...), branch_computations={%region_7.7_spmd, %region_8.10_spmd} | conditional | flops 1098260736 | bytes 51126392 | solution.py:149
  502.1 8.1 %conditional.6 = ((f32[4,4,256]{2,1,0:T(4,128)S(1)}, f32[4,4,256]{2,1,0:T(4,128)S(1)}, f32[4,4,256,128]{3,2,1,0:T(8,128)})) conditional(s32[]{:T(128)} %convert_element_type.128, (f32[4,4,256]{2,1,0:T(4,128)S(1)}, f32[4,4,256]{2,1,0:T(4,128)S(1)}, f32[4,4,256,128]{3,2,1,0:T(8,128)}) %tuple.72, (s32[512]{0:T(512)S(1)}, s32[256]{0:T(256)S(1)}, ...), branch_computations={%region_3.0_spmd, %region_4.6_spmd} | conditional | flops 1098260480 | bytes 51124340 | solution.py:146
  510.2 8.1 %conditional.7 = ((f32[4,4,256]{2,1,0:T(4,128)S(1)}, f32[4,4,256]{2,1,0:T(4,128)S(1)}, f32[4,4,256,128]{3,2,1,0:T(8,128)})) conditional(s32[]{:T(128)} %convert_element_type.129, (f32[4,4,256]{2,1,0:T(4,128)S(1)}, f32[4,4,256]{2,1,0:T(4,128)S(1)}, f32[4,4,256,128]{3,2,1,0:T(8,128)}) %tuple.74, (s32[512]{0:T(512)S(1)}, s32[]{:T(128)}, ...), branch_computations={%region_7.7_spmd, %region_8.10_spmd} | conditional | flops 1098260736 | bytes 51126392 | solution.py:149
  528.4 14.0 %convolution_convert_fusion = bf16[512,4096]{1,0:T(8,128)(2,1)} fusion(bf16[2048,4096]{1,0:T(8,128)(2,1)} %param.18, bf16[256,2048]{0,1:T(8,128)(2,1)S(1)} %bitcast.110, bf16[256,2048]{0,1:T(8,128)(2,1)S(1)} %bitcast.111), kind=kOutput, calls=%fused_computation.49 | convolution fusion | flops 8596226048 | bytes 23068672 | tf_op jit(solution)/shard_map/dot_general | solution.py:165
  542.5 71.5 %reduce-scatter.2.cloned.1.call-done = bf16[512,2048]{1,0:T(8,128)(2,1)} async-done(((bf16[512,4096]{1,0:T(8,128)(2,1)}), bf16[512,2048]{1,0:T(8,128)(2,1)}) %reduce-scatter.2.cloned.1.call-update) | async-done | bytes 2097168 | tf_op jit(solution)/shard_map/reduce_scatter | solution.py:166
  (554 shorter events, 376.8 us)
Async XLA Ops:
  6.5 60.1 %copy-start.7 = (f32[4096]{0:T(1024)S(1)}, f32[4096]{0:T(1024)}, u32[]{:S(2)}) copy-start(f32[4096]{0:T(1024)} %param.14) | copy-start | bytes 49156
  6.5 60.1 %all-gather.5.cloned.1.call-start = ((), (), s32[]{:S(2)}) async-start(), calls=%async_computation.1 | async-start | bytes 6291456 | tf_op jit(solution)/shard_map/all_gather | solution.py:63
  7.3 141.6 %all-gather.7.cloned.1.call-start = ((), (), s32[]{:S(2)}) async-start(), calls=%async_computation.2 | async-start | bytes 8912896 | tf_op jit(solution)/shard_map/all_gather | solution.py:105
  73.6 7.0 %copy-start.6 = (s32[512]{0:T(512)S(1)}, s32[512]{0:T(512)}, u32[]{:S(2)}) copy-start(s32[512]{0:T(512)} %param.19) | copy-start | bytes 6148
  73.6 150.5 %all-gather.9.cloned.1.call-start = ((), (), s32[]{:S(2)}) async-start(), calls=%async_computation.3 | async-start | bytes 8912896 | tf_op jit(solution)/shard_map/all_gather | solution.py:106
  80.3 533.7 %reduce-scatter.2.cloned.1.call-start = ((), (), s32[]{:S(2)}) async-start(), calls=%async_computation.4 | async-start | bytes 6291456 | tf_op jit(solution)/shard_map/reduce_scatter | solution.py:166
  232.2 1.8 copy-start.2
  240.3 1.8 copy-start.4
  251.6 1.8 copy-start.2
  259.7 1.8 copy-start.4
  271.0 1.8 copy-start.2
  279.1 1.8 copy-start.4
  290.4 1.8 copy-start.2
  298.5 1.8 copy-start.4
  309.8 1.8 copy-start.2
  317.9 1.8 copy-start.4
  329.2 1.8 copy-start.2
  337.3 1.8 copy-start.4
  348.6 1.8 copy-start.2
  356.7 1.8 copy-start.4
  368.1 1.8 copy-start.2
  376.1 1.8 copy-start.4
  387.5 1.8 copy-start.2
  395.5 1.8 copy-start.4
  406.9 1.8 copy-start.2
  414.9 1.8 copy-start.4
  426.3 1.8 copy-start.2
  434.4 1.8 copy-start.4
  445.7 1.8 copy-start.2
  453.8 1.8 copy-start.4
  465.1 1.8 copy-start.2
  473.2 1.8 copy-start.4
  (64 other events, 99.7 us)
Sparse Core Ops, SparseCore 0:
  8.9 57.6 all-gather.4
  73.7 75.1 all-gather.6
  151.1 72.9 all-gather.8
  542.6 71.3 reduce-scatter.1
where the time goes:
time: 625 us; the launch traced here: 621 us
  waiting for transfers between devices  233 us (37%)
  matrix products  181 us (29%)
  local copies, waits for them, and re-layouts  101 us (16%)
  other arithmetic  67.7 us (11%)
  blocking collectives  22.3 us (4%)
  between operations  13.3 us (2%)
    dot_general x30, matrix products, attend_block(): jnp.einsum('sfec,csh->sfeh', attention_weights.astype(jnp.bfloat16), valu...  95.2 us
    all_gather x1, waiting for transfers between devices, shards(): value_piece = lax.all_gather(values_flat, 'cp', axis=0, tiled=True)  75.2 us
    reduce_scatter x1, waiting for transfers between devices, shards(): lax.psum_scatter(terms.astype(jnp.bfloat16), 'tp', scatter_dimension=1, t...  71.5 us
    all_gather x1, waiting for transfers between devices, shards(): piece = lax.all_gather(hidden, 'tp', axis=1, tiled=True)  51.7 us
    reduce_sum x30, other arithmetic, attend_block(): total = total * correction_scale + jnp.sum(attention_weights, axis=-1)  51.2 us
    dot_general x30, matrix products, attend_block(): jnp.einsum('ucpm,ycm->cpuy', query_matrix, key_matrix, preferred_element_...  46.5 us
    cond x210, local copies, waits for them, and re-layouts  40.1 us
    dynamic_slice x32, local copies, waits for them, and re-layouts, inner(): lax.dynamic_slice_in_dim(value_piece, offset, tok_rows, 0)  33.5 us
  transfers between devices with their start and end apart: 4, of which 4 were waited for; matrix products, arithmetic and copies ran while one was open for 4% of the time, Pallas kernels for 0%

commit v1 on v0

v1 whole, which is shorter than its diff:
```python
import functools

import jax
import jax.numpy as jnp
from jax import lax
from jax.experimental import pallas as pl
from jax.experimental.pallas import tpu as pltpu
from jax.sharding import PartitionSpec as P

HEADS = 32
KV_HEADS = 8
HEAD_SIZE = 128
GROUP = HEADS // KV_HEADS

epsilon = 1e-05
rope_base = 500000.0
TILE = 256
KEYS = 512
LOG2E = 1.4426950408889634
SCALE = HEAD_SIZE ** (-0.5) * LOG2E
FLOOR = -1e29
MASKED = -1e30


def tables(positions):
    half = HEAD_SIZE // 2
    freqs = rope_base ** (-jnp.arange(half, dtype=jnp.float32) * 2.0 / HEAD_SIZE)
    angles = positions.astype(jnp.float32)[:, None] * freqs[None, :]
    cosine = jnp.cos(angles)
    sine = jnp.sin(angles)
    return (
        jnp.concatenate([cosine, cosine], axis=1),
        jnp.concatenate([-sine, sine], axis=1),
    )


def attend_kernel(
    bounds, q_ref, k_ref, v_ref, cos_ref, sin_ref, start_ref, out_ref, qs, m_ref, l_ref, acc_ref,
    *, tile0,
):
    tile = pl.program_id(1) + tile0
    lo, full_lo, full_hi, hi, first_pos = (bounds[tile, i] for i in range(5))
    for h in range(GROUP):
        raw = q_ref[:, h * HEAD_SIZE : (h + 1) * HEAD_SIZE]
        turned = raw * cos_ref[...] + pltpu.roll(raw, HEAD_SIZE // 2, 1) * sin_ref[...]
        qs[h] = turned.astype(jnp.bfloat16)
    m_ref[...] = jnp.full_like(m_ref, FLOOR)
    l_ref[...] = jnp.zeros_like(l_ref)
    acc_ref[...] = jnp.zeros_like(acc_ref)
    parts = KEYS // HEAD_SIZE

    def block(index, masking):
        rows = pl.ds(pl.multiple_of(index * KEYS, KEYS), KEYS)
        keys = k_ref[rows, :]
        values = v_ref[rows, :]
        if masking:
            row = lax.broadcasted_iota(jnp.int32, (TILE, HEAD_SIZE), 0)
            lane = lax.broadcasted_iota(jnp.int32, (TILE, HEAD_SIZE), 1)
            last = row + (first_pos - index * KEYS) - lane
            begin = start_ref[...] - index * KEYS - lane
            allowed = [
                (last >= c * HEAD_SIZE) & (begin <= c * HEAD_SIZE) for c in range(parts)
            ]
        for h in range(GROUP):
            scores = lax.dot_general(
                qs[h], keys, (((1,), (1,)), ((), ())), preferred_element_type=jnp.float32
            )
            pieces = [
                scores[:, c * HEAD_SIZE : (c + 1) * HEAD_SIZE] * SCALE for c in range(parts)
            ]
            if masking:
                pieces = [jnp.where(a, p, MASKED) for a, p in zip(allowed, pieces)]
            top = functools.reduce(jnp.maximum, pieces)
            old = m_ref[h]
            new = jnp.maximum(old, jnp.max(top, axis=1, keepdims=True))
            correction = jnp.exp2(old - new)
            weights = [jnp.exp2(p - new) for p in pieces]
            l_ref[h] = l_ref[h] * correction + functools.reduce(jnp.add, weights)
            rounded = jnp.concatenate([w.astype(jnp.bfloat16) for w in weights], axis=1)
            acc_ref[h] = acc_ref[h] * correction + jnp.dot(
                rounded, values, preferred_element_type=jnp.float32
            )
            m_ref[h] = new

    def loop(begin, end, masking):
        def step(index, carry):
            block(index, masking)
            return carry

        lax.fori_loop(begin, end, step, 0)

    loop(lo, full_lo, True)
    loop(full_lo, full_hi, False)
    loop(full_hi, hi, True)
    for h in range(GROUP):
        total = jnp.sum(l_ref[h], axis=1, keepdims=True)
        out_ref[:, h * HEAD_SIZE : (h + 1) * HEAD_SIZE] = (acc_ref[h] / total).astype(
            jnp.bfloat16
        )


def attend(bounds, queries, key_value, cosine, sine, starts, tile0, tiles, head0):
    count, cols = key_value.shape
    heads = cols // (2 * HEAD_SIZE)
    wide = GROUP * HEAD_SIZE
    grid_spec = pltpu.PrefetchScalarGridSpec(
        num_scalar_prefetch=1,
        grid=(heads, tiles),
        in_specs=[
            pl.BlockSpec((TILE, wide), lambda g, t, s: (t + tile0, g + head0)),
            pl.BlockSpec((count, HEAD_SIZE), lambda g, t, s: (0, g)),
            pl.BlockSpec((count, HEAD_SIZE), lambda g, t, s: (0, g + heads)),
            pl.BlockSpec((TILE, HEAD_SIZE), lambda g, t, s: (t + tile0, 0)),
            pl.BlockSpec((TILE, HEAD_SIZE), lambda g, t, s: (t + tile0, 0)),
            pl.BlockSpec((TILE, HEAD_SIZE), lambda g, t, s: (t + tile0, 0)),
        ],
        out_specs=pl.BlockSpec((TILE, wide), lambda g, t, s: (t, g)),
        scratch_shapes=[
            pltpu.VMEM((GROUP, TILE, HEAD_SIZE), jnp.bfloat16),
            pltpu.VMEM((GROUP, TILE, HEAD_SIZE), jnp.float32),
            pltpu.VMEM((GROUP, TILE, HEAD_SIZE), jnp.float32),
            pltpu.VMEM((GROUP, TILE, HEAD_SIZE), jnp.float32),
        ],
    )
    pairs = heads * GROUP * tiles * TILE * count // 2
    return pl.pallas_call(
        functools.partial(attend_kernel, tile0=tile0),
        grid_spec=grid_spec,
        out_shape=jax.ShapeDtypeStruct((tiles * TILE, heads * wide), jnp.bfloat16),
        compiler_params=pltpu.CompilerParams(
            dimension_semantics=("arbitrary", "arbitrary"), vmem_limit_bytes=40 * 2**20
        ),
        cost_estimate=pl.CostEstimate(
            flops=pairs * HEAD_SIZE * 8,
            bytes_accessed=count * cols * 2,
            transcendentals=pairs,
        ),
    )(bounds, queries, key_value, key_value, cosine, sine, starts)


def shift(array, n_tp, by):
    return lax.ppermute(array, "tp", [(i, (i + by) % n_tp) for i in range(n_tp)])


def gather_features(hidden, n_tp, rank):
    pieces = [hidden] + [shift(hidden, n_tp, by) for by in range(1, n_tp)]
    ordered = []
    for j in range(n_tp):
        which = (rank - j + n_tp) % n_tp
        piece = pieces[0]
        for by in range(1, n_tp):
            piece = jnp.where(which == by, pieces[by], piece)
        ordered.append(piece)
    return jnp.concatenate(ordered, axis=1)


def scatter_features(partial, n_tp, rank):
    width = partial.shape[1] // n_tp
    total = lax.dynamic_slice_in_dim(partial, rank * width, width, 1).astype(jnp.float32)
    for by in range(1, n_tp):
        slab = lax.dynamic_slice_in_dim(partial, (rank + by) % n_tp * width, width, 1)
        total = total + shift(slab, n_tp, by).astype(jnp.float32)
    return total.astype(jnp.bfloat16)


def shards(hidden, norm_gain, w_query, w_key, w_value, w_out, doc_ids, *, n_tp):
    tok_rows = hidden.shape[0]
    width = norm_gain.shape[0]
    local_kv = w_key.shape[1] // HEAD_SIZE
    rank = lax.axis_index("tp")
    cp_rank = lax.axis_index("cp")

    all_docs = lax.all_gather(doc_ids, "cp", axis=0, tiled=True)
    starts = jnp.sum(
        (all_docs[None, :] < doc_ids[:, None]).astype(jnp.int32), axis=1, dtype=jnp.int32
    )
    positions = cp_rank * tok_rows + jnp.arange(tok_rows, dtype=jnp.int32)
    cosine, sine = tables(positions)
    n_tiles = tok_rows // TILE
    first_pos = cp_rank * tok_rows + TILE * jnp.arange(n_tiles, dtype=jnp.int32)
    low = starts[::TILE] // KEYS
    high = (first_pos + TILE + KEYS - 1) // KEYS
    full_low = jnp.clip((starts[TILE - 1 :: TILE] + KEYS - 1) // KEYS, low, high)
    full_high = jnp.clip((first_pos + 1) // KEYS, full_low, high)
    bounds = jnp.stack([low, full_low, full_high, high, first_pos], axis=1)
    starts = jnp.broadcast_to(starts[:, None], (tok_rows, HEAD_SIZE))

    whole = gather_features(hidden, n_tp, rank).astype(jnp.float32)
    inverse_rms = lax.rsqrt(jnp.sum(whole * whole, axis=1) / width + epsilon)[:, None]
    normed = (whole * inverse_rms * norm_gain[None, :]).astype(jnp.bfloat16)

    key_raw = jnp.dot(normed, w_key, preferred_element_type=jnp.float32)
    values = jnp.dot(normed, w_value, preferred_element_type=jnp.float32).astype(jnp.bfloat16)
    key_heads = key_raw.reshape(tok_rows, local_kv, HEAD_SIZE)
    half = HEAD_SIZE // 2
    swapped = jnp.concatenate([key_heads[..., half:], key_heads[..., :half]], axis=-1)
    keys = (
        (key_heads * cosine[:, None, :] + swapped * sine[:, None, :])
        .astype(jnp.bfloat16)
        .reshape(tok_rows, local_kv * HEAD_SIZE)
    )
    cut = local_kv // 2 * HEAD_SIZE
    gathered = []
    for part in (slice(0, cut), slice(cut, None)):
        own = jnp.concatenate([keys[:, part], values[:, part]], axis=1)
        gathered.append(lax.all_gather(own, "cp", axis=0, tiled=True))
    queries = jnp.dot(normed, w_query, preferred_element_type=jnp.float32)

    args = (cosine, sine, starts)
    first = attend(bounds, queries, gathered[0], *args, 0, n_tiles, 0)
    outs = []
    for tile in range(n_tiles):
        second = attend(bounds, queries, gathered[1], *args, tile, 1, local_kv // 2)
        attended = jnp.concatenate([first[tile * TILE : (tile + 1) * TILE], second], axis=1)
        partial = jnp.dot(attended, w_out, preferred_element_type=jnp.float32)
        outs.append(scatter_features(partial.astype(jnp.bfloat16), n_tp, rank))
    return jnp.concatenate(outs, axis=0)


def solution(mesh):
    in_specs = (
        P("cp", "tp"),
        P(),
        P(None, "tp"),
        P(None, "tp"),
        P(None, "tp"),
        P("tp", None),
        P("cp"),
    )
    body = functools.partial(shards, n_tp=mesh.shape["tp"])
    return jax.shard_map(
        body, mesh=mesh, in_specs=in_specs, out_specs=P("cp", "tp"), check_vma=False
    )
```

time: 625 us -> 368 us (0.59); the launches traced: 621 us -> 374 us
  Pallas kernels: 0 us -> 162 us
  matrix products: 181 us -> 38.6 us
  waiting for transfers between devices: 233 us -> 95.7 us
  local copies, waits for them, and re-layouts: 101 us -> 27 us
  other arithmetic: 67.7 us -> 16.3 us
    pallas_call x0 -> x3, Pallas kernels: none -> 162 us  [attend(): pl.pallas_call(functools.partial(attend_kernel, tile0=tile0), grid_spec=g...]
    dot_general x64 -> x5, matrix products: 181 us -> 38.6 us  [the longest x2 17.1 us: shards(): partial = jnp.dot(attended, w_out, preferred_element_type=jnp.float32)]
    all_gather x3 -> x2, waiting for transfers between devices: 160 us -> 38 us  [shards(): gathered.append(lax.all_gather(own, 'cp', axis=0, tiled=True))]
    reduce_scatter x1 -> x0, waiting for transfers between devices: 71.5 us -> none  [shards(): lax.psum_scatter(terms.astype(jnp.bfloat16), 'tp', scatter_dimension=1, t...]
    ppermute x0 -> x3, waiting for transfers between devices: none -> 57.7 us  [shift(): lax.ppermute(array, 'tp', [(i, (i + by) % n_tp) for i in range(n_tp)])]
    reduce_sum x31 -> x2, other arithmetic: 53.2 us -> 3.02 us  [the longest x1 2.02 us: shards(): jnp.sum((all_docs[None, :] < doc_ids[:, None]).astype(jnp.int32), axis=1,...]
    dynamic_slice x48 -> x2, local copies, waits for them, and re-layouts: 50.7 us -> 1.29 us  [scatter_features(): lax.dynamic_slice_in_dim(partial, (rank + by) % n_tp * width, width, 1)]
    cond x210 -> x0, local copies, waits for them, and re-layouts: 40.1 us -> none
  transfers between devices with their start and end apart: 4 -> 5, of which waited for: 4 -> 3; matrix products, arithmetic and copies ran while one was open for 4% -> 8% of each run, Pallas kernels for 0% -> 32%
where the time goes in v1:
time: 368 us; the launch traced here: 374 us
  Pallas kernels  162 us (44%)
  waiting for transfers between devices  95.7 us (26%)
  matrix products  38.6 us (10%)
  local copies, waits for them, and re-layouts  27 us (7%)
  blocking collectives  17.1 us (5%)
  other arithmetic  16.3 us (4%)
  between operations  13.6 us (4%)
    pallas_call x3, Pallas kernels, attend(): pl.pallas_call(functools.partial(attend_kernel, tile0=tile0), grid_spec=g...  162 us
    ppermute x3, waiting for transfers between devices, shift(): lax.ppermute(array, 'tp', [(i, (i + by) % n_tp) for i in range(n_tp)])  57.7 us
    all_gather x2, waiting for transfers between devices, shards(): gathered.append(lax.all_gather(own, 'cp', axis=0, tiled=True))  38 us
    unnamed x32, local copies, waits for them, and re-layouts  18.5 us
    dot_general x2, matrix products, shards(): partial = jnp.dot(attended, w_out, preferred_element_type=jnp.float32)  17.1 us
    all_gather x1, blocking collectives, shards(): all_docs = lax.all_gather(doc_ids, 'cp', axis=0, tiled=True)  17.1 us
    dot_general x1, matrix products, shards(): queries = jnp.dot(normed, w_query, preferred_element_type=jnp.float32)  14.5 us
  transfers between devices with their start and end apart: 5, of which 3 were waited for; matrix products, arithmetic and copies ran while one was open for 8% of the time, Pallas kernels for 32%

profile of v1, /device:TPU:26, one launch (start us, length us, event | category | flops | bytes accessed | tf_op | source)
XLA Modules:
  0.0 373.7 jit_solution(12496498958028489243)
XLA Ops:
  6.5 1.5 collective-permute-start
  9.3 44.9 %collective-permute-done = bf16[512,2048]{1,0:T(8,128)(2,1)} collective-permute-done((bf16[512,2048]{1,0:T(8,128)(2,1)}, bf16[512,2048]{1,0:T(8,128)(2,1)}, u32[]{:S(2)}, u32[]{:S(2)}) %collective-permute-start) | collective-permute-done | bytes 2097184 | tf_op jit(solution)/shard_map/ppermute | solution.py:142
  54.2 2.5 broadcast_select_fusion.1
  56.8 1.0 fusion
  57.8 1.9 copy-done.12
  59.7 2.4 convolution_convert_fusion.2
  62.8 4.7 %fusion.14 = f32[512,512]{0,1:T(8,128)} fusion(bf16[4096,512]{1,0:T(8,128)(2,1)S(1)} %copy-done.13, f32[4096]{0:T(1024)S(1)} %copy-done.14, f32[512]{0:T(512)S(1)} %add_rsqrt_fusion, bf16[512,2048]{1,0:T(8,128)(2,1)S(1)} %get-tuple-element.9, bf16[512,2048]{1,0:T(8,128)(2,1)S(1)} %get-tuple-element.8), kind=kOutput, calls=%fused_computation.63 | convolution fusion | flops 2162163712 | bytes 9455616 | tf_op jit(solution)/shard_map/dot_general | solution.py:192
  67.5 2.6 copy.25
  70.1 2.1 fusion.19
  72.2 2.3 copy.30
  74.5 1.3 copy.31
  75.8 2.3 maximum_multiply_fusion
  80.6 17.1 %all-gather = s32[16,1,512]{2,1,0:T(1,128)S(1)} all-gather(s32[1,1,512]{2,1,0:T(1,128)S(1)} %bitcast.26), channel_id=1, replica_groups=mesh['cp'=16,'tp'=2] {'cp'}, dimensions={0}, use_global_device_ids=true | all-gather | bytes 34816 | tf_op jit(solution)/shard_map/all_gather | solution.py:173
  97.6 2.0 convert_reduce_fusion
  100.3 14.5 %fusion.16.q_ref = f32[512,2048]{1,0:T(8,128)} fusion(bf16[4096,2048]{1,0:T(8,128)(2,1)} %param.9, f32[4096]{0:T(1024)S(1)} %copy-done.14, f32[512]{0:T(512)S(1)} %add_rsqrt_fusion, bf16[512,2048]{1,0:T(8,128)(2,1)} %copy-done.4, bf16[512,2048]{1,0:T(8,128)(2,1)S(1)} %get-tuple-element.8), kind=kOutput, calls=%fused_computation.64 | convolution fusion | flops 8604614656 | bytes 25184256 | tf_op jit(solution)/shard_map/dot_general | solution.py:207
  114.8 38.0 %all-gather.4.cloned.1.call-done.k_ref.v_ref = bf16[8192,512]{1,0:T(8,128)(2,1)} async-done(((bf16[512,512]{1,0:T(8,128)(2,1)}), bf16[8192,512]{1,0:T(8,128)(2,1)}) %all-gather.4.cloned.1.call-update) | async-done | bytes 8388624 | tf_op jit(solution)/shard_map/all_gather | solution.py:206
  152.9 3.4 copy-done.1
  156.3 2.2 copy-done.2
  158.5 79.6 %shard_map.73 = bf16[512,1024]{1,0:T(8,128)(2,1)S(1)} custom-call(s32[2,5]{1,0:T(2,128)S(1)} %stack.17.bounds, f32[512,2048]{1,0:T(8,128)S(1)} %copy-done.2, bf16[8192,512]{1,0:T(8,128)(2,1)S(1)} %copy-done.1, bf16[8192,512]{1,0:T(8,128)(2,1)S(1)} %copy-done.1, f32[512,128]{1,0:T(8,128)S(1)} %get-tuple-element.23.cos_ref, ...), custom_call_target="tpu_custom_call" | custom-call | flops 17179869184 | bytes 8388608 | tf_op jit(solution)/shard_map/pallas_call | solution.py:126
  239.0 3.4 copy-done
  242.3 2.2 copy-done.3
  244.5 40.8 %shard_map.74 = bf16[256,1024]{1,0:T(8,128)(2,1)S(1)} custom-call(s32[2,5]{1,0:T(2,128)S(1)} %stack.17.bounds, f32[512,2048]{1,0:T(8,128)S(1)} %copy-done.3, bf16[8192,512]{1,0:T(8,128)(2,1)S(1)} %copy-done, bf16[8192,512]{1,0:T(8,128)(2,1)S(1)} %copy-done, f32[512,128]{1,0:T(8,128)S(1)} %get-tuple-element.23.cos_ref, ...), custom_call_target="tpu_custom_call" | custom-call | flops 8589934592 | bytes 8388608 | tf_op jit(solution)/shard_map/pallas_call | solution.py:126
  285.3 8.5 %convolution_convert_fusion.1 = bf16[256,4096]{1,0:T(8,128)(2,1)S(1)} fusion(bf16[2048,4096]{1,0:T(8,128)(2,1)} %param.12, bf16[256,1024]{1,0:T(8,128)(2,1)S(1)} %shard_map.74, bf16[256,1024]{1,0:T(8,128)(2,1)S(1)} %get-tuple-element.10), kind=kOutput, calls=%fused_computation.7 | convolution fusion | flops 4298113024 | bytes 19922944 | tf_op jit(solution)/shard_map/dot_general | solution.py:215
  293.8 1.2 constant_dynamic-slice_fusion.1
  295.5 1.5 collective-permute-start.1
  296.9 41.3 %shard_map.75 = bf16[256,1024]{1,0:T(8,128)(2,1)S(1)} custom-call(s32[2,5]{1,0:T(2,128)S(1)} %stack.17.bounds, f32[512,2048]{1,0:T(8,128)S(1)} %copy-done.3, bf16[8192,512]{1,0:T(8,128)(2,1)S(1)} %copy-done, bf16[8192,512]{1,0:T(8,128)(2,1)S(1)} %copy-done, f32[512,128]{1,0:T(8,128)S(1)} %get-tuple-element.23.cos_ref, ...), custom_call_target="tpu_custom_call" | custom-call | flops 8589934592 | bytes 8388608 | tf_op jit(solution)/shard_map/pallas_call | solution.py:126
  338.3 8.6 %convolution_convert_fusion = bf16[256,4096]{1,0:T(8,128)(2,1)S(1)} fusion(bf16[2048,4096]{1,0:T(8,128)(2,1)} %param.12, bf16[256,1024]{1,0:T(8,128)(2,1)S(1)} %shard_map.75, bf16[256,1024]{1,0:T(8,128)(2,1)S(1)} %copy-done.10), kind=kOutput, calls=%fused_computation.6 | convolution fusion | flops 4298113024 | bytes 19922944 | tf_op jit(solution)/shard_map/dot_general | solution.py:215
  346.9 1.3 copy-done.8
  348.9 1.6 add_convert_fusion.1
  350.5 12.7 %collective-permute-done.2 = bf16[256,2048]{1,0:T(8,128)(2,1)} collective-permute-done((bf16[256,2048]{1,0:T(8,128)(2,1)S(1)}, bf16[256,2048]{1,0:T(8,128)(2,1)}, u32[]{:S(2)}, u32[]{:S(2)}) %collective-permute-start.2) | collective-permute-done | bytes 1048608 | tf_op jit(solution)/shard_map/ppermute | solution.py:142
  363.2 2.0 add_convert_fusion
  365.3 1.6 pad_maximum_fusion.1
  (53 shorter events, 7.1 us)
Async XLA Ops:
  6.5 146.3 %all-gather.4.cloned.1.call-start = ((), (), s32[]{:S(2)}) async-start(), calls=%async_computation | async-start | bytes 8912896 | tf_op jit(solution)/shard_map/all_gather | solution.py:206
  6.5 47.7 %collective-permute-start = (bf16[512,2048]{1,0:T(8,128)(2,1)}, bf16[512,2048]{1,0:T(8,128)(2,1)}, u32[]{:S(2)}, u32[]{:S(2)}) collective-permute-start(bf16[512,2048]{1,0:T(8,128)(2,1)} %param.7), channel_id=1, source_target_pairs={{0,1},{1,0},{2,3},{3,2},{4,5},{5,4},{6,7},{7,6},{8,9},{9,8},{10,11... | collective-permute-start | bytes 6291464 | tf_op jit(solution)/shard_map/ppermute | solution.py:142
  54.2 3.6 copy-start.14
  56.7 6.1 %copy-start.4 = (bf16[512,2048]{1,0:T(8,128)(2,1)}, bf16[512,2048]{1,0:T(8,128)(2,1)S(1)}, u32[]{:S(2)}) copy-start(bf16[512,2048]{1,0:T(8,128)(2,1)S(1)} %get-tuple-element.9) | copy-start | bytes 6291460
  56.7 2.9 copy-start.12
  59.7 3.1 copy-start.13
  75.8 2.5 copy-start.5
  75.8 2.9 copy-start.9
  78.3 2.3 copy-start.11
  79.7 159.3 %all-gather.6.cloned.1.call-start = ((), (), s32[]{:S(2)}) async-start(), calls=%async_computation.1 | async-start | bytes 8912896 | tf_op jit(solution)/shard_map/all_gather | solution.py:206
  152.9 3.4 copy-start.1
  156.3 2.2 copy-start.2
  239.0 3.4 copy-start
  242.3 2.2 copy-start.3
  293.8 1.7 copy-start.6
  295.5 42.8 %copy-start.10 = (bf16[256,1024]{1,0:T(8,128)(2,1)S(1)}, bf16[256,1024]{1,0:T(8,128)(2,1)}, u32[]{:S(2)}) copy-start(bf16[256,1024]{1,0:T(8,128)(2,1)} %get-tuple-element.11) | copy-start | bytes 1572868
  295.5 53.4 %collective-permute-start.1 = (bf16[256,2048]{1,0:T(8,128)(2,1)}, bf16[256,2048]{1,0:T(8,128)(2,1)}, u32[]{:S(2)}, u32[]{:S(2)}) collective-permute-start(bf16[256,2048]{1,0:T(8,128)(2,1)} %constant_dynamic-slice_fusion.1), channel_id=1, source_target_pairs={{0,1},{1,0},{2,3},{3,2},{4,5},{5,4},{6,7},{7,6},{8,9},{9,8},{10,11... | collective-permute-start | bytes 3145736 | tf_op jit(solution)/shard_map/ppermute | solution.py:142
  338.2 10.7 %copy-start.7 = (bf16[256,4096]{1,0:T(8,128)(2,1)S(1)}, bf16[256,4096]{1,0:T(8,128)(2,1)}, u32[]{:S(2)}) copy-start(bf16[256,4096]{1,0:T(8,128)(2,1)} %copy-done.6) | copy-start | bytes 6291460
  346.9 1.3 copy-start.8
  348.3 15.0 %collective-permute-start.2 = (bf16[256,2048]{1,0:T(8,128)(2,1)S(1)}, bf16[256,2048]{1,0:T(8,128)(2,1)}, u32[]{:S(2)}, u32[]{:S(2)}) collective-permute-start(bf16[256,2048]{1,0:T(8,128)(2,1)S(1)} %constant_dynamic-slice_fusion), channel_id=1, source_target_pairs={{0,1},{1,0},{2,3},{3,2},{4,5},{5,4},{6,7},{7,6},{8,9},{9,8},{10,11... | collective-permute-start | bytes 3145736 | tf_op jit(solution)/shard_map/ppermute | solution.py:142
Sparse Core Ops, SparseCore 0:
  79.8 72.9 all-gather.3
  155.0 72.8 all-gather.5

commit v2 on v1

--- a/solution.py
+++ b/solution.py
@@ -82,21 +82,38 @@
             )
             m_ref[h] = new
 
-    def loop(begin, end, masking):
-        def step(index, carry):
-            block(index, masking)
-            return carry
-
-        lax.fori_loop(begin, end, step, 0)
-
-    loop(lo, full_lo, True)
-    loop(full_lo, full_hi, False)
-    loop(full_hi, hi, True)
+    def open_step(index, carry):
+        block(index, False)
+        return carry
+
+    def edge_step(index, carry):
+        block(jnp.where(index < full_lo, index, index + (full_hi - full_lo)), True)
+        return carry
+
+    lax.fori_loop(full_lo, full_hi, open_step, 0)
+    lax.fori_loop(lo, hi - (full_hi - full_lo), edge_step, 0)
     for h in range(GROUP):
         total = jnp.sum(l_ref[h], axis=1, keepdims=True)
         out_ref[:, h * HEAD_SIZE : (h + 1) * HEAD_SIZE] = (acc_ref[h] / total).astype(
             jnp.bfloat16
         )
+
+
+def key_value_kernel(key_ref, value_ref, cos_ref, sin_ref, *outs):
+    for h, out_ref in enumerate(outs):
+        cols = slice(h * HEAD_SIZE, (h + 1) * HEAD_SIZE)
+        raw = key_ref[:, cols]
+        turned = raw * cos_ref[...] + pltpu.roll(raw, HEAD_SIZE // 2, 1) * sin_ref[...]
+        out_ref[:, :HEAD_SIZE] = turned.astype(jnp.bfloat16)
+        out_ref[:, HEAD_SIZE:] = value_ref[:, cols].astype(jnp.bfloat16)
+
+
+def key_value_heads(key_raw, value_raw, cosine, sine):
+    rows, cols = key_raw.shape
+    shape = jax.ShapeDtypeStruct((rows, 2 * HEAD_SIZE), jnp.bfloat16)
+    return pl.pallas_call(key_value_kernel, out_shape=[shape] * (cols // HEAD_SIZE))(
+        key_raw, value_raw, cosine, sine
+    )
 
 
 def attend(bounds, queries, key_value, cosine, sine, starts, tile0, tiles, head0):
@@ -128,7 +145,7 @@
         grid_spec=grid_spec,
         out_shape=jax.ShapeDtypeStruct((tiles * TILE, heads * wide), jnp.bfloat16),
         compiler_params=pltpu.CompilerParams(
-            dimension_semantics=("arbitrary", "arbitrary"), vmem_limit_bytes=40 * 2**20
+            dimension_semantics=("arbitrary", "arbitrary"), vmem_limit_bytes=60 * 2**20
         ),
         cost_estimate=pl.CostEstimate(
             flops=pairs * HEAD_SIZE * 8,
@@ -190,28 +207,22 @@
     normed = (whole * inverse_rms * norm_gain[None, :]).astype(jnp.bfloat16)
 
     key_raw = jnp.dot(normed, w_key, preferred_element_type=jnp.float32)
-    values = jnp.dot(normed, w_value, preferred_element_type=jnp.float32).astype(jnp.bfloat16)
-    key_heads = key_raw.reshape(tok_rows, local_kv, HEAD_SIZE)
-    half = HEAD_SIZE // 2
-    swapped = jnp.concatenate([key_heads[..., half:], key_heads[..., :half]], axis=-1)
-    keys = (
-        (key_heads * cosine[:, None, :] + swapped * sine[:, None, :])
-        .astype(jnp.bfloat16)
-        .reshape(tok_rows, local_kv * HEAD_SIZE)
-    )
-    cut = local_kv // 2 * HEAD_SIZE
-    gathered = []
-    for part in (slice(0, cut), slice(cut, None)):
-        own = jnp.concatenate([keys[:, part], values[:, part]], axis=1)
-        gathered.append(lax.all_gather(own, "cp", axis=0, tiled=True))
+    value_raw = jnp.dot(normed, w_value, preferred_element_type=jnp.float32)
+    gathered = [
+        lax.all_gather(own, "cp", axis=0, tiled=True)
+        for own in key_value_heads(key_raw, value_raw, cosine, sine)
+    ]
     queries = jnp.dot(normed, w_query, preferred_element_type=jnp.float32)
 
     args = (cosine, sine, starts)
-    first = attend(bounds, queries, gathered[0], *args, 0, n_tiles, 0)
+    first = [
+        attend(bounds, queries, gathered[g], *args, 0, n_tiles, g) for g in range(local_kv - 1)
+    ]
     outs = []
     for tile in range(n_tiles):
-        second = attend(bounds, queries, gathered[1], *args, tile, 1, local_kv // 2)
-        attended = jnp.concatenate([first[tile * TILE : (tile + 1) * TILE], second], axis=1)
+        last = attend(bounds, queries, gathered[-1], *args, tile, 1, local_kv - 1)
+        rows = slice(tile * TILE, (tile + 1) * TILE)
+        attended = jnp.concatenate([part[rows] for part in first] + [last], axis=1)
         partial = jnp.dot(attended, w_out, preferred_element_type=jnp.float32)
         outs.append(scatter_features(partial.astype(jnp.bfloat16), n_tp, rank))
     return jnp.concatenate(outs, axis=0)

time: 368 us -> 375 us (1.019)
  the two profiles are of different devices: /device:TPU:26 before, /device:TPU:19 now
where the time goes in v2:
time: 375 us
  Pallas kernels  165 us (44%)
  waiting for transfers between devices  111 us (30%)
  matrix products  42.1 us (11%)
  blocking collectives  16.3 us (4%)
  between operations  13.3 us (4%)
  other arithmetic  12.8 us (3%)
  local copies, waits for them, and re-layouts  11 us (3%)
    pallas_call x5, Pallas kernels, attend(): pl.pallas_call(functools.partial(attend_kernel, tile0=tile0), grid_spec=g...  162 us
    ppermute x3, waiting for transfers between devices, shift(): lax.ppermute(array, 'tp', [(i, (i + by) % n_tp) for i in range(n_tp)])  65 us
    all_gather x4, waiting for transfers between devices, shards(): lax.all_gather(own, 'cp', axis=0, tiled=True)  44.5 us
    dot_general x2, matrix products, shards(): partial = jnp.dot(attended, w_out, preferred_element_type=jnp.float32)  20.7 us
    all_gather x1, blocking collectives, shards(): all_docs = lax.all_gather(doc_ids, 'cp', axis=0, tiled=True)  16.3 us
    dot_general x1, matrix products, shards(): queries = jnp.dot(normed, w_query, preferred_element_type=jnp.float32)  14.5 us
  transfers between devices with their start and end apart: 7, of which 6 were waited for; matrix products, arithmetic and copies ran while one was open for 10% of the time, Pallas kernels for 38%

profile of v2, /device:TPU:19, one launch (start us, length us, event | category | flops | bytes accessed | tf_op | source)
XLA Modules:
  0.0 374.8 jit_solution(2755213120794920621)
XLA Ops:
  6.5 1.2 collective-permute-start
  9.8 43.6 %collective-permute-done = bf16[512,2048]{1,0:T(8,128)(2,1)} collective-permute-done((bf16[512,2048]{1,0:T(8,128)(2,1)}, bf16[512,2048]{1,0:T(8,128)(2,1)}, u32[]{:S(2)}, u32[]{:S(2)}) %collective-permute-start) | collective-permute-done | bytes 2097184 | tf_op jit(solution)/shard_map/ppermute | solution.py:159
  53.4 2.5 broadcast_select_fusion.1
  55.9 1.0 fusion
  56.9 1.9 copy-done.5
  58.8 3.4 fusion.22.key_ref
  62.3 3.4 fusion.20.value_ref
  65.7 3.0 shard_map.73
  70.7 16.3 %all-gather = s32[16,1,512]{2,1,0:T(1,128)S(1)} all-gather(s32[1,1,512]{2,1,0:T(1,128)S(1)} %bitcast.12), channel_id=1, replica_groups=mesh['cp'=16,'tp'=2] {'cp'}, dimensions={0}, use_global_device_ids=true | all-gather | bytes 34816 | tf_op jit(solution)/shard_map/all_gather | solution.py:190
  87.0 2.0 convert_reduce_fusion
  90.2 14.5 %fusion.24.q_ref = f32[512,2048]{1,0:T(8,128)} fusion(bf16[4096,2048]{1,0:T(8,128)(2,1)} %param.9, f32[4096]{0:T(1024)S(1)} %copy-done.7, f32[512]{0:T(512)S(1)} %add_rsqrt_fusion, bf16[512,2048]{1,0:T(8,128)(2,1)} %copy-done, bf16[512,2048]{1,0:T(8,128)(2,1)S(1)} %get-tuple-element.16), kind=kOutput, calls=%fused_computation.66 | convolution fusion | flops 8604614656 | bytes 25184256 | tf_op jit(solution)/shard_map/dot_general | solution.py:215
  104.7 15.5 %all-gather.6.cloned.1.call-done.k_ref.v_ref = bf16[8192,256]{1,0:T(8,128)(2,1)} async-done(((bf16[512,256]{1,0:T(8,128)(2,1)}), bf16[8192,256]{1,0:T(8,128)(2,1)}) %all-gather.6.cloned.1.call-update) | async-done | bytes 4194320 | tf_op jit(solution)/shard_map/all_gather | solution.py:212
  121.1 39.5 %shard_map.74 = bf16[512,512]{1,0:T(8,128)(2,1)} custom-call(s32[2,5]{1,0:T(2,128)} %stack.17.bounds, f32[512,2048]{1,0:T(8,128)} %fusion.24.q_ref, bf16[8192,256]{1,0:T(8,128)(2,1)} %all-gather.6.cloned.1.call-done.k_ref.v_ref, bf16[8192,256]{1,0:T(8,128)(2,1)} %all-gather.6.cloned.1.call-done.k_ref.v_ref, f32[512,128]{1,0:T(8,128)} %get-tuple-element.29.cos_ref, ...), custom_call_target="tpu_custom_call" | custom-call | flops 8589934592 | bytes 4194304 | tf_op jit(solution)/shard_map/pallas_call | solution.py:143
  160.6 1.1 fusion.26
  161.7 9.7 %all-gather.8.cloned.1.call-done.k_ref.v_ref = bf16[8192,256]{1,0:T(8,128)(2,1)} async-done(((bf16[512,256]{1,0:T(8,128)(2,1)}), bf16[8192,256]{1,0:T(8,128)(2,1)}) %all-gather.8.cloned.1.call-update) | async-done | bytes 4194320 | tf_op jit(solution)/shard_map/all_gather | solution.py:212
  171.4 39.5 %shard_map.75 = bf16[512,512]{1,0:T(8,128)(2,1)} custom-call(s32[2,5]{1,0:T(2,128)} %stack.17.bounds, f32[512,2048]{1,0:T(8,128)} %fusion.24.q_ref, bf16[8192,256]{1,0:T(8,128)(2,1)} %all-gather.8.cloned.1.call-done.k_ref.v_ref, bf16[8192,256]{1,0:T(8,128)(2,1)} %all-gather.8.cloned.1.call-done.k_ref.v_ref, f32[512,128]{1,0:T(8,128)} %get-tuple-element.29.cos_ref, ...), custom_call_target="tpu_custom_call" | custom-call | flops 8589934592 | bytes 4194304 | tf_op jit(solution)/shard_map/pallas_call | solution.py:143
  210.9 1.8 fusion.27
  212.7 9.8 %all-gather.10.cloned.1.call-done.k_ref.v_ref = bf16[8192,256]{1,0:T(8,128)(2,1)} async-done(((bf16[512,256]{1,0:T(8,128)(2,1)}), bf16[8192,256]{1,0:T(8,128)(2,1)}) %all-gather.10.cloned.1.call-update) | async-done | bytes 4194320 | tf_op jit(solution)/shard_map/all_gather | solution.py:212
  222.5 39.8 %shard_map.76 = bf16[512,512]{1,0:T(8,128)(2,1)} custom-call(s32[2,5]{1,0:T(2,128)} %stack.17.bounds, f32[512,2048]{1,0:T(8,128)} %fusion.24.q_ref, bf16[8192,256]{1,0:T(8,128)(2,1)} %all-gather.10.cloned.1.call-done.k_ref.v_ref, bf16[8192,256]{1,0:T(8,128)(2,1)} %all-gather.10.cloned.1.call-done.k_ref.v_ref, f32[512,128]{1,0:T(8,128)} %get-tuple-element.29.cos_ref, ...), custom_call_target="tpu_custom_call" | custom-call | flops 8589934592 | bytes 4194304 | tf_op jit(solution)/shard_map/pallas_call | solution.py:143
  262.2 1.8 fusion.28
  264.0 9.4 %all-gather.12.cloned.1.call-done.k_ref.v_ref = bf16[8192,256]{1,0:T(8,128)(2,1)} async-done(((bf16[512,256]{1,0:T(8,128)(2,1)}), bf16[8192,256]{1,0:T(8,128)(2,1)}) %all-gather.12.cloned.1.call-update) | async-done | bytes 4194320 | tf_op jit(solution)/shard_map/all_gather | solution.py:212
  273.5 21.6 %shard_map.77 = bf16[256,512]{1,0:T(8,128)(2,1)} custom-call(s32[2,5]{1,0:T(2,128)} %stack.17.bounds, f32[512,2048]{1,0:T(8,128)} %fusion.24.q_ref, bf16[8192,256]{1,0:T(8,128)(2,1)} %all-gather.12.cloned.1.call-done.k_ref.v_ref, bf16[8192,256]{1,0:T(8,128)(2,1)} %all-gather.12.cloned.1.call-done.k_ref.v_ref, f32[512,128]{1,0:T(8,128)} %get-tuple-element.29.cos_ref, ...), custom_call_target="tpu_custom_call" | custom-call | flops 4294967296 | bytes 4194304 | tf_op jit(solution)/shard_map/pallas_call | solution.py:143
  295.0 10.4 %convolution_convert_fusion.1 = bf16[256,4096]{1,0:T(8,128)(2,1)S(1)} fusion(bf16[2048,4096]{1,0:T(8,128)(2,1)} %param.12, bf16[256,512]{1,0:T(8,128)(2,1)} %shard_map.77, bf16[256,512]{1,0:T(8,128)(2,1)S(1)} %get-tuple-element.22, bf16[256,512]{1,0:T(8,128)(2,1)S(1)} %get-tuple-element.20, bf16[256,512]{1,0:T(8,128)(2,1)S(1)} %get-tuple-element.18), kind=kOutput, calls=%fused_computation.7 | convolution fusion | flops 4300210176 | bytes 19922944 | tf_op jit(solution)/shard_map/dot_general | solution.py:226
  305.5 1.3 collective-permute-start.1
  306.8 21.8 %shard_map.78 = bf16[256,512]{1,0:T(8,128)(2,1)} custom-call(s32[2,5]{1,0:T(2,128)} %stack.17.bounds, f32[512,2048]{1,0:T(8,128)} %fusion.24.q_ref, bf16[8192,256]{1,0:T(8,128)(2,1)} %all-gather.12.cloned.1.call-done.k_ref.v_ref, bf16[8192,256]{1,0:T(8,128)(2,1)} %all-gather.12.cloned.1.call-done.k_ref.v_ref, f32[512,128]{1,0:T(8,128)} %get-tuple-element.29.cos_ref, ...), custom_call_target="tpu_custom_call" | custom-call | flops 4294967296 | bytes 4194304 | tf_op jit(solution)/shard_map/pallas_call | solution.py:143
  328.6 10.4 %convolution_convert_fusion = bf16[256,4096]{1,0:T(8,128)(2,1)S(1)} fusion(bf16[2048,4096]{1,0:T(8,128)(2,1)} %param.12, bf16[256,512]{1,0:T(8,128)(2,1)} %shard_map.78, bf16[256,512]{1,0:T(8,128)(2,1)S(1)} %copy-done.3, bf16[256,512]{1,0:T(8,128)(2,1)S(1)} %copy-done.2, bf16[256,512]{1,0:T(8,128)(2,1)S(1)} %get-tuple-element.19), kind=kOutput, calls=%fused_computation.6 | convolution fusion | flops 4300210176 | bytes 19922944 | tf_op jit(solution)/shard_map/dot_general | solution.py:226
  339.0 1.3 copy-done.1
  340.3 1.1 constant_dynamic-slice_fusion
  341.7 1.6 add_convert_fusion.1
  343.3 21.4 %collective-permute-done.2 = bf16[256,2048]{1,0:T(8,128)(2,1)} collective-permute-done((bf16[256,2048]{1,0:T(8,128)(2,1)}, bf16[256,2048]{1,0:T(8,128)(2,1)}, u32[]{:S(2)}, u32[]{:S(2)}) %collective-permute-start.2) | collective-permute-done | bytes 1048608 | tf_op jit(solution)/shard_map/ppermute | solution.py:159
  364.7 2.0 add_convert_fusion
  366.7 1.6 pad_maximum_fusion.1
  (39 shorter events, 6.4 us)
Async XLA Ops:
  6.5 113.7 %all-gather.6.cloned.1.call-start = ((), (), s32[]{:S(2)}) async-start(), calls=%async_computation | async-start | bytes 4456448 | tf_op jit(solution)/shard_map/all_gather | solution.py:212
  6.5 46.8 %collective-permute-start = (bf16[512,2048]{1,0:T(8,128)(2,1)}, bf16[512,2048]{1,0:T(8,128)(2,1)}, u32[]{:S(2)}, u32[]{:S(2)}) collective-permute-start(bf16[512,2048]{1,0:T(8,128)(2,1)} %param.7), channel_id=1, source_target_pairs={{0,1},{1,0},{2,3},{3,2},{4,5},{5,4},{6,7},{7,6},{8,9},{9,8},{10,11... | collective-permute-start | bytes 6291464 | tf_op jit(solution)/shard_map/ppermute | solution.py:159
  53.4 3.6 copy-start.7
  55.9 6.4 %copy-start = (bf16[512,2048]{1,0:T(8,128)(2,1)}, bf16[512,2048]{1,0:T(8,128)(2,1)S(1)}, u32[]{:S(2)}) copy-start(bf16[512,2048]{1,0:T(8,128)(2,1)S(1)} %get-tuple-element.17) | copy-start | bytes 6291460
  55.9 2.9 copy-start.5
  58.8 3.4 copy-start.6
  62.3 8.5 %copy-start.4 = (s32[512]{0:T(512)S(1)}, s32[512]{0:T(512)}, u32[]{:S(2)}) copy-start(s32[512]{0:T(512)} %param.13) | copy-start | bytes 6148
  68.7 102.7 %all-gather.8.cloned.1.call-start = ((), (), s32[]{:S(2)}) async-start(), calls=%async_computation.1 | async-start | bytes 4456448 | tf_op jit(solution)/shard_map/all_gather | solution.py:212
  69.4 153.1 %all-gather.10.cloned.1.call-start = ((), (), s32[]{:S(2)}) async-start(), calls=%async_computation.2 | async-start | bytes 4456448 | tf_op jit(solution)/shard_map/all_gather | solution.py:212
  70.2 203.3 %all-gather.12.cloned.1.call-start = ((), (), s32[]{:S(2)}) async-start(), calls=%async_computation.3 | async-start | bytes 4456448 | tf_op jit(solution)/shard_map/all_gather | solution.py:212
  305.5 23.1 %copy-start.2 = (bf16[256,512]{1,0:T(8,128)(2,1)S(1)}, bf16[256,512]{1,0:T(8,128)(2,1)}, u32[]{:S(2)}) copy-start(bf16[256,512]{1,0:T(8,128)(2,1)} %get-tuple-element.21) | copy-start | bytes 786436
  305.5 23.1 %copy-start.3 = (bf16[256,512]{1,0:T(8,128)(2,1)S(1)}, bf16[256,512]{1,0:T(8,128)(2,1)}, u32[]{:S(2)}) copy-start(bf16[256,512]{1,0:T(8,128)(2,1)} %get-tuple-element.23) | copy-start | bytes 786436
  305.5 36.1 %collective-permute-start.1 = (bf16[256,2048]{1,0:T(8,128)(2,1)S(1)}, bf16[256,2048]{1,0:T(8,128)(2,1)}, u32[]{:S(2)}, u32[]{:S(2)}) collective-permute-start(bf16[256,2048]{1,0:T(8,128)(2,1)S(1)} %constant_dynamic-slice_fusion.1), channel_id=1, source_target_pairs={{0,1},{1,0},{2,3},{3,2},{4,5},{5,4},{6,7},{7,6},{8,9},{9,8},{10,11... | collective-permute-start | bytes 3145736 | tf_op jit(solution)/shard_map/ppermute | solution.py:159
  339.0 1.3 copy-start.1
  341.4 23.3 %collective-permute-start.2 = (bf16[256,2048]{1,0:T(8,128)(2,1)}, bf16[256,2048]{1,0:T(8,128)(2,1)}, u32[]{:S(2)}, u32[]{:S(2)}) collective-permute-start(bf16[256,2048]{1,0:T(8,128)(2,1)} %constant_dynamic-slice_fusion), channel_id=1, source_target_pairs={{0,1},{1,0},{2,3},{3,2},{4,5},{5,4},{6,7},{7,6},{8,9},{9,8},{10,11... | collective-permute-start | bytes 3145736 | tf_op jit(solution)/shard_map/ppermute | solution.py:159
Sparse Core Ops, SparseCore 0:
  68.8 51.4 all-gather.5
  122.4 48.9 all-gather.7
  173.5 48.8 all-gather.9
  224.5 48.9 all-gather.11
